TPU v7x, 8 devices: a whole 2x2x1 slice. The times are simulated.
8 devices in a mesh: rep: 2 (over y, z), dp: 4 (over x, core).
Axes of the slice: x: 2, y: 2, z: 1, core: 2. Of those that a mesh axis runs over, the one named last changes fastest.
Arguments:
- x: bfloat16 [8, 2048, 1280], P(('rep', 'dp')), parts along dimension 0
- dy: bfloat16 [8, 2048, 1280], P(('rep', 'dp')), parts along dimension 0
- w_gate: bfloat16 [2, 1280, 4480], P(None, 'dp')
- w_up: bfloat16 [2, 1280, 4480], P(None, 'dp')
- w_down: bfloat16 [2, 4480, 1280], P(None, 'dp')
- m_w_gate: float32 [2, 1280, 4480], P(None, 'dp')
- m_w_up: float32 [2, 1280, 4480], P(None, 'dp')
- m_w_down: float32 [2, 4480, 1280], P(None, 'dp')
- v_w_gate: float32 [2, 1280, 4480], P(None, 'dp')
- v_w_up: float32 [2, 1280, 4480], P(None, 'dp')
- v_w_down: float32 [2, 4480, 1280], P(None, 'dp')
Outputs:
- output 1: bfloat16 [4, 1280, 4480], P('rep', 'dp'), parts along dimension 0
- output 2: bfloat16 [4, 1280, 4480], P('rep', 'dp'), parts along dimension 0
- output 3: bfloat16 [4, 4480, 1280], P('rep', 'dp'), parts along dimension 0
- output 4: float32 [4, 1280, 4480], P('rep', 'dp'), parts along dimension 0
- output 5: float32 [4, 1280, 4480], P('rep', 'dp'), parts along dimension 0
- output 6: float32 [4, 4480, 1280], P('rep', 'dp'), parts along dimension 0
- output 7: float32 [4, 1280, 4480], P('rep', 'dp'), parts along dimension 0
- output 8: float32 [4, 1280, 4480], P('rep', 'dp'), parts along dimension 0
- output 9: float32 [4, 4480, 1280], P('rep', 'dp'), parts along dimension 0
There are 2 independent parts. A program takes and returns all parts, laid end to end along the dimension named above; an argument that names none is the same for every part.
All inputs are finite; a program needn't handle non-finite values.
Results may differ from a plain program's by a relative error of at most 0.022.
Values are sent between devices in bfloat16 or wider.
A program may use at most 2 GiB of HBM per device.

v0:
```python
import jax
import jax.numpy as jnp
from jax import lax
from jax.sharding import PartitionSpec as P

NAMES = ("w_gate", "w_up", "w_down")


def matmul(a, w):
    return jnp.dot(a, w, preferred_element_type=jnp.float32).astype(jnp.bfloat16)


def normed(h):
    wide = h.astype(jnp.float32)
    scale = lax.rsqrt(jnp.mean(wide**2, -1, keepdims=True) + 1e-6)
    return (wide * scale).astype(jnp.bfloat16)


def layer(h, w):
    a = normed(h)
    gate = jnp.dot(a, w["w_gate"], preferred_element_type=jnp.float32)
    up = jnp.dot(a, w["w_up"], preferred_element_type=jnp.float32)
    return h + matmul((jax.nn.silu(gate) * up).astype(jnp.bfloat16), w["w_down"])


def adamw(w, m, v, g):
    m = 0.9 * m + 0.1 * g
    v = 0.95 * v + 0.05 * g * g
    step = m * lax.rsqrt(v + 1e-8) + 0.1 * w
    return (w - 0.02 * step).astype(jnp.bfloat16), m, v


def solution(mesh):
    def fetched(weights, number):
        return {name: lax.all_gather(w[number], "dp", axis=0, tiled=True) for name, w in zip(NAMES, weights, strict=True)}

    def step(x, dy, *arrays):
        weights, m, v = (arrays[i : i + 3] for i in (0, 3, 6))
        layers = weights[0].shape[0]
        h, kept = x[0], []
        for number in range(layers):
            kept.append(h)
            h = layer(h, fetched(weights, number))
        by_h, mine = dy[0], [None] * layers
        for number in reversed(range(layers)):
            _, back = jax.vjp(lambda w, h: layer(h, w), fetched(weights, number), kept[number])
            by_w, by_h = back(by_h)
            mine[number] = [lax.psum_scatter(by_w[name], "dp", scatter_dimension=0, tiled=True) for name in NAMES]
        gradients = [jnp.stack([mine[number][i] for number in range(layers)]).astype(jnp.float32) for i in range(3)]
        new = [adamw(w.astype(jnp.float32), m, v, g) for w, m, v, g in zip(weights, m, v, gradients, strict=True)]
        return tuple(one[which] for which in range(3) for one in new)

    states, cut = P(("rep", "dp"), None, None), P(None, "dp", None)
    return jax.shard_map(
        step,
        mesh=mesh,
        in_specs=(states, states) + (cut,) * 9,
        out_specs=(P("rep", "dp", None),) * 9,
        check_vma=False,
    )
```

profile of v0, /device:TPU:0, one launch (start us, length us, event | category | flops | bytes accessed | tf_op | source)
XLA Modules:
  0.0 1217.1 jit_solution(5806396579228861484)
XLA Ops:
  7.2 0.0 all-gather.13.cloned.1.call-start
  7.2 5.6 fusion.97
  12.8 0.0 all-gather.13.cloned.1.call-update
  12.8 0.0 all-gather.15.cloned.1.call-start
  12.9 5.6 fusion.96
  18.5 0.0 all-gather.15.cloned.1.call-update
  18.5 0.0 all-gather.17.cloned.1.call-start
  18.5 5.6 fusion.95
  24.1 0.0 all-gather.17.cloned.1.call-update
  24.1 0.0 all-gather.21.cloned.1.call-start
  24.2 0.5 all-gather.21.cloned.1.call-update
  24.7 0.0 all-gather.23.cloned.1.call-start
  24.8 0.5 all-gather.23.cloned.1.call-update
  25.3 0.0 all-gather.19.cloned.1.call-start
  25.3 0.5 all-gather.19.cloned.1.call-update
  25.9 0.0 reduce-scatter.11.cloned.1.call-start
  25.9 7.9 copy.20
  33.8 3.6 fusion.49
  37.4 7.9 copy.21
  45.3 44.0 %all-gather.13.cloned.1.call-done = bf16[1,1280,4480]{2,1,0:T(8,128)(2,1)} async-done(((bf16[1,320,4480]{2,1,0:T(8,128)(2,1)}), bf16[1,1280,4480]{2,1,0:T(8,128)(2,1)}) %all-gather.13.cloned.1.call-update) | async-done | bytes 11468816 | tf_op jit(solution)/shard_map/all_gather | solution.py:35
  89.3 32.0 %fusion.47 = f32[2048,4480]{1,0:T(8,128)} fusion(bf16[1,1280,4480]{2,1,0:T(8,128)(2,1)} %all-gather.13.cloned.1.call-done, bf16[1,2048,1280]{1,2,0:T(8,128)(2,1)} %copy.20, f32[2048]{0:T(1024)S(1)} %add_rsqrt_fusion), kind=kOutput, calls=%fused_computation.78 | convolution fusion | flops 23495966720 | bytes 53420032 | tf_op jit(solution)/shard_map/dot_general | solution.py:21
  121.3 43.6 %all-gather.15.cloned.1.call-done = bf16[1,1280,4480]{2,1,0:T(8,128)(2,1)} async-done(((bf16[1,320,4480]{2,1,0:T(8,128)(2,1)}), bf16[1,1280,4480]{2,1,0:T(8,128)(2,1)}) %all-gather.15.cloned.1.call-update) | async-done | bytes 11468816 | tf_op jit(solution)/shard_map/all_gather | solution.py:35
  165.0 45.3 %multiply_convert_fusion.1 = (bf16[2048,4480]{1,0:T(8,128)(2,1)}, f32[2048,4480]{1,0:T(8,128)}) fusion(f32[2048,4480]{1,0:T(8,128)} %fusion.47, bf16[1,1280,4480]{2,1,0:T(8,128)(2,1)} %all-gather.15.cloned.1.call-done, bf16[1,2048,1280]{1,2,0:T(8,128)(2,1)} %copy.20, f32[2048]{0:T(1024)S(1)} %add_rsqrt_fusion), kind=kOutput, calls=%fused_computation.17 | convolution fusion | flops 23551016960 | bytes 108470272 | tf_op jit(solution)/shard_map/dot_general | solution.py:22
  210.3 30.4 %all-gather.17.cloned.1.call-done = bf16[1,4480,1280]{2,1,0:T(8,128)(2,1)} async-done(((bf16[1,1120,1280]{2,1,0:T(8,128)(2,1)}), bf16[1,4480,1280]{2,1,0:T(8,128)(2,1)}) %all-gather.17.cloned.1.call-update) | async-done | bytes 11468816 | tf_op jit(solution)/shard_map/all_gather | solution.py:35
  240.6 33.0 %fusion.53 = (f32[2048]{0:T(1024)S(1)}, bf16[2048,1280]{0,1:T(8,128)(2,1)}) fusion(bf16[2048,4480]{1,0:T(8,128)(2,1)} %get-tuple-element.24, bf16[1,4480,1280]{2,1,0:T(8,128)(2,1)} %all-gather.17.cloned.1.call-done, bf16[1,2048,1280]{1,2,0:T(8,128)(2,1)} %copy.20), kind=kOutput, calls=%fused_computation.84 | convolution fusion | flops 23501207552 | bytes 40312832 | tf_op jit(solution)/shard_map/dot_general | solution.py:10
  273.6 42.5 %all-gather.21.cloned.1.call-done = bf16[1,4480,1280]{2,1,0:T(8,128)(2,1)} async-done(((bf16[1,1120,1280]{2,1,0:T(8,128)(2,1)}), bf16[1,4480,1280]{2,1,0:T(8,128)(2,1)}) %all-gather.21.cloned.1.call-update) | async-done | bytes 11468816 | tf_op jit(solution)/shard_map/all_gather | solution.py:35
  316.1 31.6 %convolution_convert_fusion.1 = bf16[2048,4480]{1,0:T(8,128)(2,1)} fusion(bf16[1,4480,1280]{2,1,0:T(8,128)(2,1)} %all-gather.21.cloned.1.call-done, bf16[1,2048,1280]{2,1,0:T(8,128)(2,1)} %param.12), kind=kOutput, calls=%fused_computation.26 | convolution fusion | flops 23497277440 | bytes 35061760 | tf_op jit(solution)/shard_map/transpose(jvp())/dot_general | solution.py:10
  347.7 43.9 %all-gather.23.cloned.1.call-done = bf16[1,1280,4480]{2,1,0:T(8,128)(2,1)} async-done(((bf16[1,320,4480]{2,1,0:T(8,128)(2,1)}), bf16[1,1280,4480]{2,1,0:T(8,128)(2,1)}) %all-gather.23.cloned.1.call-update) | async-done | bytes 11468816 | tf_op jit(solution)/shard_map/all_gather | solution.py:35
  391.6 31.9 %fusion.34 = f32[2048,4480]{1,0:T(8,128)} fusion(bf16[1,1280,4480]{2,1,0:T(8,128)(2,1)} %all-gather.23.cloned.1.call-done, bf16[2048,1280]{0,1:T(8,128)(2,1)} %get-tuple-element.27, f32[2048]{0:T(1024)S(1)} %fusion.83), kind=kOutput, calls=%fused_computation.65 | convolution fusion | flops 23495966720 | bytes 53420032 | tf_op jit(solution)/shard_map/jvp()/dot_general | solution.py:22
  423.6 43.6 %all-gather.19.cloned.1.call-done = bf16[1,1280,4480]{2,1,0:T(8,128)(2,1)} async-done(((bf16[1,320,4480]{2,1,0:T(8,128)(2,1)}), bf16[1,1280,4480]{2,1,0:T(8,128)(2,1)}) %all-gather.19.cloned.1.call-update) | async-done | bytes 11468816 | tf_op jit(solution)/shard_map/all_gather | solution.py:35
  467.1 54.1 %fusion.2 = (bf16[2048,4480]{1,0:T(8,128)(2,1)}, f32[2048,4480]{1,0:T(8,128)}) fusion(f32[2048,4480]{1,0:T(8,128)} %fusion.34, bf16[2048,4480]{1,0:T(8,128)(2,1)} %convolution_convert_fusion.1, bf16[1,1280,4480]{2,1,0:T(8,128)(2,1)} %all-gather.19.cloned.1.call-done, bf16[2048,1280]{0,1:T(8,128)(2,1)} %get-tuple-element.27, f32[2048]{0:T(1024)S(1)} %fusion.83), kind=kOutput, calls=%fused_computation.8 | convolution fusion | flops 23606067200 | bytes 126820352 | tf_op jit(solution)/shard_map/jvp()/dot_general | solution.py:21
  521.2 35.4 %fusion.59 = bf16[2048,1280]{0,1:T(8,128)(2,1)} fusion(bf16[1,1280,4480]{2,1,0:T(8,128)(2,1)} %all-gather.23.cloned.1.call-done, bf16[2048,4480]{1,0:T(8,128)(2,1)} %convolution_convert_fusion.1, f32[2048,4480]{1,0:T(8,128)} %get-tuple-element.29), kind=kOutput, calls=%fused_computation.88 | convolution fusion | flops 23545774080 | bytes 71761920 | tf_op jit(solution)/shard_map/transpose(jvp())/dot_general | solution.py:22
  556.6 34.1 %fusion.55 = (f32[2048]{0:T(1024)S(1)}, bf16[2048,1280]{0,1:T(8,128)(2,1)}) fusion(bf16[2048,1280]{0,1:T(8,128)(2,1)} %get-tuple-element.27, bf16[2048,1280]{0,1:T(8,128)(2,1)} %fusion.59, bf16[2048,4480]{1,0:T(8,128)(2,1)} %get-tuple-element.28, bf16[1,1280,4480]{2,1,0:T(8,128)(2,1)} %all-gather.19.cloned.1.call-done), kind=kOutput, calls=%fused_computation.86 | convolution fusion | flops 23501207552 | bytes 45555712 | tf_op jit(solution)/shard_map/transpose(jvp())/dot_general | solution.py:21
  590.8 12.4 %fusion.72 = bf16[2048,1280]{0,1:T(8,128)(2,1)} fusion(bf16[2048,1280]{0,1:T(8,128)(2,1)} %get-tuple-element.27, bf16[2048,1280]{0,1:T(8,128)(2,1)} %get-tuple-element.31, bf16[1,2048,1280]{1,2,0:T(8,128)(2,1)} %copy.21, f32[2048]{0:T(1024)S(1)} %multiply_multiply_fusion.3, f32[2048]{0:T(1024)S(1)} %fusion.83), kind=kLoop, calls=%fused_computation.95 | loop fusion | flops 18350080 | bytes 20987904 | tf_op jit(solution)/shard_map/transpose(jvp())/add_any | solution.py:14
  603.2 31.6 %convolution_convert_fusion = bf16[2048,4480]{1,0:T(8,128)(2,1)} fusion(bf16[2048,1280]{0,1:T(8,128)(2,1)} %fusion.72, bf16[1,4480,1280]{2,1,0:T(8,128)(2,1)} %all-gather.17.cloned.1.call-done), kind=kOutput, calls=%fused_computation.25 | convolution fusion | flops 23497277440 | bytes 35061760 | tf_op jit(solution)/shard_map/transpose(jvp())/dot_general | solution.py:10
  634.8 37.4 %fusion.17 = bf16[1280,4480]{1,0:T(8,128)(2,1)} fusion(bf16[2048,4480]{1,0:T(8,128)(2,1)} %convolution_convert_fusion, f32[2048,4480]{1,0:T(8,128)} %fusion.47, bf16[1,2048,1280]{1,2,0:T(8,128)(2,1)} %copy.20, f32[2048]{0:T(1024)S(1)} %copy-done.6), kind=kOutput, calls=%fused_computation.24 | convolution fusion | flops 23556751360 | bytes 71770112 | tf_op jit(solution)/shard_map/transpose(jvp())/dot_general | solution.py:22
  672.2 0.0 reduce-scatter.11.cloned.1.call-update
  672.2 0.0 reduce-scatter.13.cloned.1.call-start
  672.3 0.6 copy-done.1
  672.9 37.4 %fusion.13 = bf16[1280,4480]{1,0:T(8,128)(2,1)} fusion(bf16[2048,4480]{1,0:T(8,128)(2,1)} %convolution_convert_fusion.1, bf16[2048,1280]{0,1:T(8,128)(2,1)} %get-tuple-element.27, f32[2048]{0:T(1024)S(1)} %copy-done.1, f32[2048,4480]{1,0:T(8,128)} %get-tuple-element.29), kind=kOutput, calls=%fused_computation.22 | convolution fusion | flops 23556751360 | bytes 71770112 | tf_op jit(solution)/shard_map/transpose(jvp())/dot_general | solution.py:22
  710.3 0.0 reduce-scatter.13.cloned.1.call-update
  710.3 0.0 reduce-scatter.17.cloned.1.call-start
  710.3 38.9 %convolution_convert_fusion.2 = bf16[4480,1280]{1,0:T(8,128)(2,1)} fusion(f32[2048,4480]{1,0:T(8,128)} %fusion.34, bf16[1,2048,1280]{2,1,0:T(8,128)(2,1)} %param.12, f32[2048,4480]{1,0:T(8,128)} %get-tuple-element.29), kind=kOutput, calls=%fused_computation.27 | convolution fusion | flops 23548887040 | bytes 90112000 | tf_op jit(solution)/shard_map/transpose(jvp())/dot_general | solution.py:10
  749.2 0.0 reduce-scatter.17.cloned.1.call-update
  749.2 0.0 reduce-scatter.15.cloned.1.call-start
  749.3 30.1 %convolution_convert_fusion.3 = bf16[4480,1280]{1,0:T(8,128)(2,1)} fusion(bf16[2048,4480]{1,0:T(8,128)(2,1)} %get-tuple-element.24, bf16[2048,1280]{0,1:T(8,128)(2,1)} %fusion.72), kind=kOutput, calls=%fused_computation.28 | convolution fusion | flops 23493836800 | bytes 35061760 | tf_op jit(solution)/shard_map/transpose(jvp())/dot_general | solution.py:10
  779.3 0.0 reduce-scatter.15.cloned.1.call-update
  779.4 0.0 reduce-scatter.7.cloned.1.call-start
  779.4 0.6 copy-done.7
  780.0 44.3 %fusion.14 = bf16[1280,4480]{1,0:T(8,128)(2,1)} fusion(f32[2048,4480]{1,0:T(8,128)} %fusion.47, f32[2048,4480]{1,0:T(8,128)} %get-tuple-element.25, bf16[2048,4480]{1,0:T(8,128)(2,1)} %convolution_convert_fusion, bf16[1,2048,1280]{1,2,0:T(8,128)(2,1)} %copy.20, f32[2048]{0:T(1024)S(1)} %copy-done.7), kind=kOutput, calls=%fused_computation.23 | convolution fusion | flops 23602626560 | bytes 108470272 | tf_op jit(solution)/shard_map/transpose(jvp())/dot_general | solution.py:21
  824.4 0.0 reduce-scatter.7.cloned.1.call-update
  824.4 0.0 reduce-scatter.9.cloned.1.call-start
  824.4 0.6 copy-done.2
  825.1 31.3 %convolution_convert_fusion.4 = bf16[1280,4480]{1,0:T(8,128)(2,1)} fusion(bf16[2048,4480]{1,0:T(8,128)(2,1)} %get-tuple-element.28, bf16[2048,1280]{0,1:T(8,128)(2,1)} %get-tuple-element.27, f32[2048]{0:T(1024)S(1)} %copy-done.2), kind=kOutput, calls=%fused_computation.29 | convolution fusion | flops 23495966720 | bytes 35069952 | tf_op jit(solution)/shard_map/transpose(jvp())/dot_general | solution.py:21
  856.4 0.0 reduce-scatter.9.cloned.1.call-update
  856.4 0.0 reduce-scatter.11.cloned.1.call-done
  856.4 0.0 reduce-scatter.13.cloned.1.call-done
  856.4 20.4 %fusion.25 = (bf16[2,320,4480]{2,1,0:T(8,128)(2,1)}, f32[2,320,4480]{2,1,0:T(8,128)}, f32[2,320,4480]{2,1,0:T(8,128)}) fusion(bf16[2,320,4480]{2,1,0:T(8,128)(2,1)} %param.14, bf16[1,320,4480]{2,1,0:T(8,128)(2,1)} %bitcast.76, bf16[1,320,4480]{2,1,0:T(8,128)(2,1)} %bitcast.75, f32[2,320,4480]{2,1,0:T(8,128)} %param.20, f32[2,320,4480]{2,1,0:T(8,128)} %param.17), kind=kLoop, calls=%fused_computation.56 | loop fusion | flops 54476800 | bytes 63078400 | tf_op jit(solution)/shard_map/convert_element_type | solution.py:30
  876.8 52.7 %reduce-scatter.17.cloned.1.call-done = bf16[1120,1280]{1,0:T(8,128)(2,1)} async-done(((bf16[4480,1280]{1,0:T(8,128)(2,1)}), bf16[1120,1280]{1,0:T(8,128)(2,1)}) %reduce-scatter.17.cloned.1.call-update) | async-done | bytes 2867216 | tf_op jit(solution)/shard_map/reduce_scatter | solution.py:48
  929.5 86.3 %reduce-scatter.15.cloned.1.call-done = bf16[1120,1280]{1,0:T(8,128)(2,1)} async-done(((bf16[4480,1280]{1,0:T(8,128)(2,1)}), bf16[1120,1280]{1,0:T(8,128)(2,1)}) %reduce-scatter.15.cloned.1.call-update) | async-done | bytes 2867216 | tf_op jit(solution)/shard_map/reduce_scatter | solution.py:48
  1015.8 23.5 %fusion.29 = (bf16[2,1120,1280]{2,1,0:T(8,128)(2,1)}, f32[2,1120,1280]{2,1,0:T(8,128)}, f32[2,1120,1280]{2,1,0:T(8,128)}) fusion(bf16[2,1120,1280]{2,1,0:T(8,128)(2,1)} %param.15, bf16[1,1120,1280]{2,1,0:T(8,128)(2,1)} %bitcast.77, bf16[1,1120,1280]{2,1,0:T(8,128)(2,1)} %bitcast.78, f32[2,1120,1280]{2,1,0:T(8,128)} %param.21, f32[2,1120,1280]{2,1,0:T(8,128)} %param.18), kind=kLoop, calls=%fused_computation.60 | loop fusion | flops 54476800 | bytes 63078400 | tf_op jit(solution)/shard_map/convert_element_type | solution.py:30
  1039.3 63.5 %reduce-scatter.7.cloned.1.call-done = bf16[320,4480]{1,0:T(8,128)(2,1)} async-done(((bf16[1280,4480]{1,0:T(8,128)(2,1)}), bf16[320,4480]{1,0:T(8,128)(2,1)}) %reduce-scatter.7.cloned.1.call-update) | async-done | bytes 2867216 | tf_op jit(solution)/shard_map/reduce_scatter | solution.py:48
  1102.8 86.8 %reduce-scatter.9.cloned.1.call-done = bf16[320,4480]{1,0:T(8,128)(2,1)} async-done(((bf16[1280,4480]{1,0:T(8,128)(2,1)}), bf16[320,4480]{1,0:T(8,128)(2,1)}) %reduce-scatter.9.cloned.1.call-update) | async-done | bytes 2867216 | tf_op jit(solution)/shard_map/reduce_scatter | solution.py:48
  1189.7 20.4 %fusion.21 = (bf16[2,320,4480]{2,1,0:T(8,128)(2,1)}, f32[2,320,4480]{2,1,0:T(8,128)}, f32[2,320,4480]{2,1,0:T(8,128)}) fusion(bf16[2,320,4480]{2,1,0:T(8,128)(2,1)} %param.13, bf16[1,320,4480]{2,1,0:T(8,128)(2,1)} %bitcast.80, bf16[1,320,4480]{2,1,0:T(8,128)(2,1)} %bitcast.79, f32[2,320,4480]{2,1,0:T(8,128)} %param.19, f32[2,320,4480]{2,1,0:T(8,128)} %param.16), kind=kLoop, calls=%fused_computation.52 | loop fusion | flops 54476800 | bytes 63078400 | tf_op jit(solution)/shard_map/convert_element_type | solution.py:30
  (16 shorter events, 0.1 us)
Async XLA Ops:
  7.2 82.2 %all-gather.13.cloned.1.call-start = ((), (), s32[]{:S(2)}) async-start(), calls=%async_computation.12 | async-start | bytes 14336000 | tf_op jit(solution)/shard_map/all_gather | solution.py:35
  12.8 152.2 %all-gather.15.cloned.1.call-start = ((), (), s32[]{:S(2)}) async-start(), calls=%async_computation.13 | async-start | bytes 14336000 | tf_op jit(solution)/shard_map/all_gather | solution.py:35
  18.5 222.2 %all-gather.17.cloned.1.call-start = ((), (), s32[]{:S(2)}) async-start(), calls=%async_computation.14 | async-start | bytes 14336000 | tf_op jit(solution)/shard_map/all_gather | solution.py:35
  24.1 292.0 %all-gather.21.cloned.1.call-start = ((), (), s32[]{:S(2)}) async-start(), calls=%async_computation.16 | async-start | bytes 14336000 | tf_op jit(solution)/shard_map/all_gather | solution.py:35
  24.7 366.9 %all-gather.23.cloned.1.call-start = ((), (), s32[]{:S(2)}) async-start(), calls=%async_computation.17 | async-start | bytes 14336000 | tf_op jit(solution)/shard_map/all_gather | solution.py:35
  25.3 441.9 %all-gather.19.cloned.1.call-start = ((), (), s32[]{:S(2)}) async-start(), calls=%async_computation.15 | async-start | bytes 14336000 | tf_op jit(solution)/shard_map/all_gather | solution.py:35
  25.9 830.5 %reduce-scatter.11.cloned.1.call-start = ((), (), s32[]{:S(2)}) async-start(), calls=%async_computation.8 | async-start | bytes 14336000 | tf_op jit(solution)/shard_map/reduce_scatter | solution.py:48
  37.4 127.6 %copy-start.5 = (f32[2048]{0:T(1024)}, f32[2048]{0:T(1024)S(1)}, u32[]{:S(2)}) copy-start(f32[2048]{0:T(1024)S(1)} %add_rsqrt_fusion) | copy-start | bytes 24580
  273.6 74.1 %copy-start.3 = (f32[2048]{0:T(1024)}, f32[2048]{0:T(1024)S(1)}, u32[]{:S(2)}) copy-start(f32[2048]{0:T(1024)S(1)} %get-tuple-element.26) | copy-start | bytes 24580
  273.6 317.2 %copy-start = (f32[2048]{0:T(1024)}, f32[2048]{0:T(1024)S(1)}, u32[]{:S(2)}) copy-start(f32[2048]{0:T(1024)S(1)} %fusion.83) | copy-start | bytes 24580
  556.6 34.1 %copy-start.4 = (f32[2048]{0:T(1024)S(1)}, f32[2048]{0:T(1024)}, u32[]{:S(2)}) copy-start(f32[2048]{0:T(1024)} %copy-done.3) | copy-start | bytes 24580
  603.2 31.6 %copy-start.6 = (f32[2048]{0:T(1024)S(1)}, f32[2048]{0:T(1024)}, u32[]{:S(2)}) copy-start(f32[2048]{0:T(1024)} %copy-done.5) | copy-start | bytes 24580
  672.2 0.7 copy-start.1
  672.2 184.2 %reduce-scatter.13.cloned.1.call-start = ((), (), s32[]{:S(2)}) async-start(), calls=%async_computation.9 | async-start | bytes 14336000 | tf_op jit(solution)/shard_map/reduce_scatter | solution.py:48
  710.3 219.3 %reduce-scatter.17.cloned.1.call-start = ((), (), s32[]{:S(2)}) async-start(), calls=%async_computation.11 | async-start | bytes 14336000 | tf_op jit(solution)/shard_map/reduce_scatter | solution.py:48
  749.2 266.6 %reduce-scatter.15.cloned.1.call-start = ((), (), s32[]{:S(2)}) async-start(), calls=%async_computation.10 | async-start | bytes 14336000 | tf_op jit(solution)/shard_map/reduce_scatter | solution.py:48
  779.3 0.7 copy-start.7
  779.4 323.4 %reduce-scatter.7.cloned.1.call-start = ((), (), s32[]{:S(2)}) async-start(), calls=%async_computation.6 | async-start | bytes 14336000 | tf_op jit(solution)/shard_map/reduce_scatter | solution.py:48
  824.4 0.7 copy-start.2
  824.4 365.3 %reduce-scatter.9.cloned.1.call-start = ((), (), s32[]{:S(2)}) async-start(), calls=%async_computation.7 | async-start | bytes 14336000 | tf_op jit(solution)/shard_map/reduce_scatter | solution.py:48
Sparse Core Ops, SparseCore 0:
  12.9 76.3 all-gather.12
  91.4 73.5 all-gather.14
  167.1 73.5 all-gather.16
  242.6 73.5 all-gather.20
  318.1 73.5 all-gather.22
  393.6 73.5 all-gather.18
  672.3 83.7 reduce-scatter.10
  759.3 83.7 reduce-scatter.12
  845.7 83.7 reduce-scatter.16
  932.0 83.7 reduce-scatter.14
  1019.0 83.7 reduce-scatter.6
  1105.8 83.7 reduce-scatter.8
where the time goes:
time: 1220 us
  matrix products  548 us (45%)
  waiting for transfers between devices  539 us (44%)
  other arithmetic  80.2 us (7%)
  local copies, waits for them, and re-layouts  34.4 us (3%)
  between operations  14.5 us (1%)
    reduce_scatter x6, waiting for transfers between devices, step(): lax.psum_scatter(by_w[name], 'dp', scatter_dimension=0, tiled=True)  289 us
    all_gather x6, waiting for transfers between devices, fetched(): lax.all_gather(w[number], 'dp', axis=0, tiled=True)  248 us
    dot_general x5, matrix products, layer(): gate = jnp.dot(a, w['w_gate'], preferred_element_type=jnp.float32)  196 us
    dot_general x5, matrix products, layer(): up = jnp.dot(a, w['w_up'], preferred_element_type=jnp.float32)  187 us
    dot_general x5, matrix products, matmul(): jnp.dot(a, w, preferred_element_type=jnp.float32).astype(jnp.bfloat16)  165 us
    convert_element_type x3, other arithmetic, adamw(): return ((w - 0.02 * step).astype(jnp.bfloat16), m, v)  64.2 us
  transfers between devices with their start and end apart: 12, of which 10 were waited for; matrix products, arithmetic and copies ran while one was open for 35% of the time, Pallas kernels for 0%

commit v1 on v0

v1 whole, which is shorter than its diff:
```python
import jax
import jax.numpy as jnp
from jax import lax
from jax.experimental import pallas as pl
from jax.experimental.pallas import tpu as pltpu
from jax.sharding import PartitionSpec as P


MESH = pl.DeviceIdType.MESH
HBM = pl.BlockSpec(memory_space=pltpu.HBM)
TILE = 512
CHUNK = 1024
BLOCK = 256
LAYERS = 2
COUNT = 3 * LAYERS


def cuts(rows):
    units = rows // 16
    small = max(units // 10, 1)
    middle = units - 2 * small
    sizes = [small] + [middle // 4 + (k < middle % 4) for k in range(4)] + [small]
    starts = [sum(sizes[:k]) for k in range(len(sizes))]
    return [(16 * a, 16 * b) for a, b in zip(starts, sizes)]


PIECES = 6
AHEAD = 8
LEAD = 2


class Gather:
    def __init__(self, blocks, wholes, sems):
        self.blocks, self.wholes = blocks, wholes
        self.own_s, self.own_r, self.x_s, self.x_r, self.y_s, self.y_r, self.c_s, self.c_r, self.e_s, self.e_r = sems
        y, d = lax.axis_index("rep"), lax.axis_index("dp")
        self.y, self.x, self.c = y, d // 2, d % 2
        self.over_x, self.over_y, self.over_c = (y, (1 - self.x) * 2 + self.c), (1 - y, d), (y, self.x * 2 + 1 - self.c)

    def barrier(self):
        sem = pltpu.get_barrier_semaphore()
        for device in (self.over_x, self.over_y, self.over_c):
            pl.semaphore_signal(sem, inc=1, device_id=device, device_id_type=MESH)
        pl.semaphore_wait(sem, 3)

    def mine(self, j):
        rows = self.blocks[j].shape[0]
        return self.wholes[j].at[pl.ds((self.x * 2 + self.c) * rows, rows)]

    def own(self, j):
        return pltpu.make_async_remote_copy(
            self.blocks[j], self.mine(j), self.own_s.at[j], self.own_r.at[j], device_id=self.over_c, device_id_type=MESH
        )

    def piece(self, j, k, chip, half):
        rows = self.blocks[j].shape[0]
        start, size = cuts(rows // 2)[k]
        return self.wholes[j].at[pl.ds((chip * 2 + self.c) * rows + half * (rows // 2) + start, size)]

    def first(self, j, k):
        rows = self.blocks[j].shape[0]
        start, size = cuts(rows // 2)[k]
        source = self.blocks[j].at[pl.ds(self.y * (rows // 2) + start, size)]
        n = j * PIECES + k
        return pltpu.make_async_remote_copy(
            source, self.piece(j, k, self.x, self.y), self.x_s.at[n], self.x_r.at[n], device_id=self.over_x, device_id_type=MESH
        )

    def send(self, j, k, half, sems, device):
        at, n = self.piece(j, k, 1 - self.x, half), j * PIECES + k
        return pltpu.make_async_remote_copy(at, at, sems[0].at[n], sems[1].at[n], device_id=device, device_id_type=MESH)

    def second(self, j, k):
        return self.send(j, k, self.y, (self.y_s, self.y_r), self.over_y)

    def hand(self, j, k):
        return self.send(j, k, self.y, (self.c_s, self.c_r), self.over_c)

    def hand_late(self, j, k):
        return self.send(j, k, 1 - self.y, (self.e_s, self.e_r), self.over_c)

    def start(self):
        self.barrier()
        for n in range(AHEAD):
            self.first(*divmod(n, PIECES)).start()
        for j in range(len(self.blocks)):
            self.own(j).start()

    def pass_on(self, n):
        at = divmod(n, PIECES)
        self.first(*at).wait()
        if n + AHEAD < len(self.blocks) * PIECES:
            self.first(*divmod(n + AHEAD, PIECES)).start()
        self.second(*at).start()
        self.hand(*at).start()
        if n >= 1:
            self.pass_late(n - 1)

    def pass_late(self, n):
        j, k = divmod(n, PIECES)
        self.send(j, k, 1 - self.y, (self.y_s, self.y_r), self.over_y).wait_recv()
        self.hand_late(j, k).start()

    def ready(self, j):
        self.own(j).wait_recv()
        for k in range(PIECES):
            self.hand(j, k).wait_recv()
            self.hand_late(j, k).wait_recv()

    def finish(self):
        for j in range(len(self.blocks)):
            self.own(j).wait_send()
            for k in range(PIECES):
                self.second(j, k).wait_send()
                self.hand(j, k).wait_send()
                self.hand_late(j, k).wait_send()


def scaled(wide):
    return (wide * lax.rsqrt(jnp.mean(wide * wide, -1, keepdims=True) + 1e-6)).astype(jnp.bfloat16)


def dot(a, b):
    return jnp.dot(a, b, preferred_element_type=jnp.float32)


def chunks(rows, body):
    @pl.loop(0, rows // CHUNK)
    def _(n):
        body(pl.ds(pl.multiple_of(n * CHUNK, CHUNK), CHUNK))


def over_columns(body, ins, outs, tick):
    columns = ins[0].shape[1]
    main = columns // TILE
    steps = pl.cdiv(columns, TILE)
    for start, count, width in ((0, main, TILE), (main * TILE, steps - main, columns - main * TILE)):
        if count == 0:
            continue

        def tile(*refs, start=start, width=width):
            n = pl.program_id(0)
            tick(start // TILE + n, steps)
            body(pl.ds(pl.multiple_of(start + n * width, 128), width), *refs)

        specs = [pl.BlockSpec((r.shape[0], width), lambda n: (0, n)) for r in ins + outs]
        parts = [r.at[:, pl.ds(start, count * width)] for r in ins + outs]
        pltpu.emit_pipeline(tile, grid=(count,), in_specs=specs[: len(ins)], out_specs=specs[len(ins) :])(*parts)


def forward_kernel(x_ref, wg, wu, wd, g0, u0, d0, g1, u1, d1, a0_ref, a1_ref, h1_ref, gate0, up0, hid0, gate1, up1, hid1, act, sem, out_sem, *sems):
    blocks = [w.at[n] for n in range(LAYERS) for w in (wg, wu, wd)]
    wholes = [g0, u0, d0, g1, u1, d1]
    g = Gather(blocks, wholes, sems)
    g.start()

    def ticks(j):
        def tick(n, steps):
            for k in range(PIECES):
                piece = j * PIECES + LEAD + k
                if piece < COUNT * PIECES:

                    @pl.when(n == (k + 1) * (steps - 1) // PIECES)
                    def _(piece=piece):
                        g.pass_on(piece)

        return tick

    def place_own(wide_block, tall_block):
        for j in range(COUNT):
            g.pass_on(j)
            held = tall_block if j % 3 == 2 else wide_block
            for source, target in ((blocks[j], held), (held, g.mine(j))):
                move = pltpu.make_async_copy(source, target, sem.at[1])
                move.start()
                move.wait()

    copy = pltpu.make_async_copy(x_ref, act, sem.at[0])
    copy.start()
    copy.wait()
    chunks(act.shape[0], lambda rows: act.__setitem__((rows, slice(None)), scaled(act[rows, :].astype(jnp.float32))))
    copy = pltpu.make_async_copy(act, a0_ref, sem.at[0])
    copy.start()
    pl.run_scoped(place_own, pltpu.VMEM(blocks[0].shape, blocks[0].dtype), pltpu.VMEM(blocks[2].shape, blocks[2].dtype))
    for n in range(COUNT, PIECES + LEAD):
        g.pass_on(n)
    g.ready(0)
    copy.wait()

    def gate_and_up(j, w_gate, w_up, gate_ref, up_ref, hid_ref):
        def within(gate):
            def gate_tile(columns, w):
                def some(rows):
                    gate[rows, columns] = dot(act[rows, :], w[...])

                chunks(act.shape[0], some)
                pltpu.make_async_copy(gate.at[:, columns], gate_ref.at[:, columns], out_sem.at[0]).start()

            def up_tile(columns, w, up_out, hid):
                def some(rows):
                    up = dot(act[rows, :], w[...])
                    up_out[rows, :] = up
                    hid[rows, :] = (jax.nn.silu(gate[rows, columns]) * up).astype(jnp.bfloat16)

                chunks(act.shape[0], some)

            over_columns(gate_tile, [w_gate], [], ticks(j))
            g.ready(j)
            over_columns(up_tile, [w_up], [up_ref, hid_ref], ticks(j + 1))
            pltpu.make_async_copy(gate, gate_ref, out_sem.at[0]).wait()

        pl.run_scoped(within, pltpu.VMEM(gate_ref.shape, gate_ref.dtype))

    gate_and_up(1, g0, u0, gate0, up0, hid0)
    g.ready(2)

    def down(w_down):
        load = pltpu.make_async_copy(d0, w_down, sem.at[0])
        load.start()
        load.wait()
        steps = act.shape[0] // BLOCK

        def some(hid, x, h1, a1):
            ticks(3)(pl.program_id(0), steps)
            wide = x[...].astype(jnp.float32) + dot(hid[...], w_down[...]).astype(jnp.bfloat16).astype(jnp.float32)
            h = wide.astype(jnp.bfloat16)
            h1[...] = h
            a1[...] = scaled(h.astype(jnp.float32))

        rows = lambda r: pl.BlockSpec((BLOCK, r.shape[1]), lambda n: (n, 0))
        refs = (hid0, x_ref, h1_ref, a1_ref)
        pltpu.emit_pipeline(some, grid=(steps,), in_specs=[rows(r) for r in refs[:2]], out_specs=[rows(r) for r in refs[2:]])(*refs)

    pl.run_scoped(down, pltpu.VMEM(d0.shape, d0.dtype))
    copy = pltpu.make_async_copy(a1_ref, act, sem.at[0])
    copy.start()
    g.ready(3)
    copy.wait()
    gate_and_up(4, g1, u1, gate1, up1, hid1)
    g.pass_late(COUNT * PIECES - 1)
    g.ready(5)
    g.finish()


def forward(x, w_gate, w_up, w_down):
    (tokens, d), ff = x.shape, w_gate.shape[2]
    bf16, f32 = jnp.bfloat16, jnp.float32
    shape = jax.ShapeDtypeStruct
    wholes = [shape((d, ff), bf16), shape((d, ff), bf16), shape((ff, d), bf16)] * LAYERS
    states = [shape((tokens, d), bf16)] * 3
    hidden = [shape((tokens, ff), f32), shape((tokens, ff), f32), shape((tokens, ff), bf16)] * LAYERS
    pieces = COUNT * PIECES
    out = pl.pallas_call(
        forward_kernel,
        name="forward",
        out_shape=wholes + states + hidden,
        in_specs=[HBM] * 4,
        out_specs=[HBM] * (len(wholes) + len(states) + len(hidden)),
        scratch_shapes=[pltpu.VMEM((tokens, d), bf16), pltpu.SemaphoreType.DMA((2,)), pltpu.SemaphoreType.DMA((1,))]
        + [pltpu.SemaphoreType.DMA((n,)) for n in (COUNT, COUNT) + (pieces,) * 8],
        compiler_params=pltpu.CompilerParams(collective_id=0, has_side_effects=True, vmem_limit_bytes=63 * 2**20),
    )(x, w_gate, w_up, w_down)
    return out[:COUNT], out[COUNT : COUNT + 3], out[COUNT + 3 :]


def normed(h):
    return scaled(h.astype(jnp.float32))


def adamw(w, m, v, g):
    m = 0.9 * m + 0.1 * g
    v = 0.95 * v + 0.05 * g * g
    step = m * lax.rsqrt(v + 1e-8) + 0.1 * w
    return (w - 0.02 * step).astype(jnp.bfloat16), m, v


CORES = [[0, 1], [2, 3]]
OVER_X = [(0, 2), (1, 3), (2, 0), (3, 1)]


def summed(g):
    g = g.reshape(2, 2, g.shape[0] // 4, g.shape[1])
    return lax.psum_scatter(g, "dp", scatter_dimension=1, axis_index_groups=CORES)


def backward_hidden(by_h, w_down, gate, up):
    by_hid = lax.dot_general(by_h, w_down, (((1,), (1,)), ((), ())), preferred_element_type=jnp.float32).astype(jnp.bfloat16).astype(jnp.float32)
    s = jax.nn.sigmoid(gate)
    by_up = by_hid * (gate * s)
    by_gate = by_hid * up * (s * (1 + gate * (1 - s)))
    return by_gate.astype(jnp.bfloat16), by_up.astype(jnp.bfloat16)


def to_weight(a, b):
    return lax.dot_general(a, b, (((0,), (0,)), ((), ())), preferred_element_type=jnp.float32).astype(jnp.bfloat16)


def to_input(a, w):
    return lax.dot_general(a, w, (((1,), (1,)), ((), ())), preferred_element_type=jnp.float32)


def solution(mesh):
    def step(x, dy, *arrays):
        weights, m, v = (arrays[i : i + 3] for i in (0, 3, 6))
        chip = lax.axis_index("dp") // 2
        x, dy = x[0], dy[0]
        wholes, (a0, a1, h1), hidden = forward(x, *weights)
        (_, _, down0, gate1, up1, down1) = wholes
        summing, got = {}, {}

        def send(name, g):
            summing[name] = summed(g)

        def travel(name, *later):
            both, *later = lax.optimization_barrier((summing[name], *later))
            theirs, ours = (lax.dynamic_index_in_dim(both, at, 0, False) for at in (1 - chip, chip))
            got[name] = (ours, lax.ppermute(theirs, "dp", OVER_X))
            return later

        g, u, hid = hidden[3:]
        send("d1", to_weight(hid, dy))
        by_gate, by_up = backward_hidden(dy, down1, g, u)
        by_gate, by_up = travel("d1", by_gate, by_up)
        send("g1", to_weight(a1, by_gate))
        send("u1", to_weight(a1, by_up))
        by_gate, by_up = travel("g1", by_gate, by_up)
        by_a = (to_input(by_gate, gate1) + to_input(by_up, up1)).astype(jnp.bfloat16)
        by_h = dy + jax.vjp(normed, h1)[1](by_a)[0]
        (by_h,) = travel("u1", by_h)
        g, u, hid = hidden[:3]
        send("d0", to_weight(hid, by_h))
        by_gate, by_up = backward_hidden(by_h, down0, g, u)
        by_gate, by_up = travel("d0", by_gate, by_up)
        send("g0", to_weight(a0, by_gate))
        by_u0 = to_weight(a0, by_up)
        send("u0", by_u0)
        travel("g0", by_u0)
        travel("u0")

        new = []
        for name, w, m, v in zip("gud", weights, m, v):
            total = [(ours.astype(jnp.float32) + other.astype(jnp.float32)).astype(jnp.bfloat16) for ours, other in (got[name + "0"], got[name + "1"])]
            new.append(adamw(w.astype(jnp.float32), m, v, jnp.stack(total).astype(jnp.float32)))
        return tuple(one[which] for which in range(3) for one in new)

    states, cut = P(("rep", "dp"), None, None), P(None, "dp", None)
    return jax.shard_map(
        step,
        mesh=mesh,
        in_specs=(states, states) + (cut,) * 9,
        out_specs=(P("rep", "dp", None),) * 9,
        check_vma=False,
    )
```

time: 1220 us -> 1080 us (0.89)
  Pallas kernels: 0 us -> 269 us
  waiting for transfers between devices: 539 us -> 291 us
  matrix products: 548 us -> 354 us
  local copies, waits for them, and re-layouts: 34.4 us -> 47 us
    ppermute x0 -> x6, waiting for transfers between devices: none -> 291 us  [travel(): got[name] = (ours, lax.ppermute(theirs, 'dp', OVER_X))]
    reduce_scatter x6, waiting for transfers between devices: 289 us -> 0.05 us  [summed(): lax.psum_scatter(g, 'dp', scatter_dimension=1, axis_index_groups=CORES)]
    pallas_call x0 -> x1, Pallas kernels: none -> 269 us  [forward(): pl.pallas_call(forward_kernel, name='forward', out_shape=wholes + states...]
    all_gather x6 -> x0, waiting for transfers between devices: 248 us -> none  [fetched(): lax.all_gather(w[number], 'dp', axis=0, tiled=True)]
    dot_general x15 -> x10, matrix products: 548 us -> 354 us  [the longest x6 178 us: to_weight(): lax.dot_general(a, b, (((0,), (0,)), ((), ())), preferred_element_type=jn...]
    reshape x0 -> x6, local copies, waits for them, and re-layouts: none -> 27.9 us  [summed(): g = g.reshape(2, 2, g.shape[0] // 4, g.shape[1])]
    squeeze x0 -> x6, local copies, waits for them, and re-layouts: none -> 19.1 us  [travel(): lax.dynamic_index_in_dim(both, at, 0, False)]
    another operation x0 -> x6, other arithmetic: none -> 18.9 us  [step(): jnp.stack(total).astype(jnp.float32)]
  transfers between devices with their start and end apart: 12 -> 12, of which waited for: 10 -> 6; matrix products, arithmetic and copies ran while one was open for 35% -> 31% of each run, Pallas kernels for 0% -> 0%
where the time goes in v1:
time: 1080 us; the launch traced here: 1070 us
  matrix products  354 us (33%)
  waiting for transfers between devices  291 us (27%)
  Pallas kernels  269 us (25%)
  other arithmetic  88.2 us (8%)
  local copies, waits for them, and re-layouts  47 us (4%)
  between operations  14.8 us (1%)
    ppermute x6, waiting for transfers between devices, travel(): got[name] = (ours, lax.ppermute(theirs, 'dp', OVER_X))  291 us
    pallas_call x1, Pallas kernels, forward(): pl.pallas_call(forward_kernel, name='forward', out_shape=wholes + states...  269 us
    dot_general x6, matrix products, to_weight(): lax.dot_general(a, b, (((0,), (0,)), ((), ())), preferred_element_type=jn...  178 us
    dot_general x2, matrix products, backward_hidden(): lax.dot_general(by_h, w_down, (((1,), (1,)), ((), ())), preferred_element...  107 us
    dot_general x2, matrix products, to_input(): lax.dot_general(a, w, (((1,), (1,)), ((), ())), preferred_element_type=jn...  68.8 us
    convert_element_type x3, other arithmetic, adamw(): return ((w - 0.02 * step).astype(jnp.bfloat16), m, v)  59.5 us
    reshape x6, local copies, waits for them, and re-layouts, summed(): g = g.reshape(2, 2, g.shape[0] // 4, g.shape[1])  27.9 us
  transfers between devices with their start and end apart: 12, of which 6 were waited for; matrix products, arithmetic and copies ran while one was open for 31% of the time, Pallas kernels for 0%

profile of v1, /device:TPU:0, one launch (start us, length us, event | category | flops | bytes accessed | tf_op | source)
XLA Modules:
  0.0 1070.7 jit_solution(9153237447996191398)
XLA Ops:
  7.2 0.0 reduce-scatter.7.cloned.1.call-start
  7.2 268.9 %forward.1 = (bf16[1280,4480]{1,0:T(8,128)(2,1)}, bf16[1280,4480]{1,0:T(8,128)(2,1)}, bf16[4480,1280]{1,0:T(8,128)(2,1)}, bf16[1280,4480]{1,0:T(8,128)(2,1)}, bf...) custom-call(bf16[2048,1280]{1,0:T(8,128)(2,1)} %bitcast.116, ...), custom_call_target="tpu_custom_call" | custom-call | tf_op jit(solution)/shard_map/forward/pallas_call | solution.py:253
  276.1 28.8 %convolution_convert_fusion.7 = bf16[4480,1280]{1,0:T(8,128)(2,1)S(1)} fusion(bf16[2048,4480]{1,0:T(8,128)(2,1)} %get-tuple-element.37, bf16[1,2048,1280]{2,1,0:T(8,128)(2,1)} %param.12), kind=kOutput, calls=%fused_computation.19 | convolution fusion | flops 23493836800 | bytes 35061760 | tf_op jit(solution)/shard_map/dot_general | solution.py:295
  304.9 4.6 copy.20
  309.6 0.0 reduce-scatter.7.cloned.1.call-update
  309.6 0.0 reduce-scatter.11.cloned.1.call-start
  309.6 53.3 %fusion.5 = (bf16[2048,4480]{1,0:T(8,128)(2,1)}, bf16[2048,4480]{1,0:T(8,128)(2,1)}) fusion(f32[2048,4480]{1,0:T(8,128)} %get-tuple-element.40, f32[2048,4480]{1,0:T(8,128)} %get-tuple-element.39, bf16[4480,1280]{1,0:T(8,128)(2,1)} %get-tuple-element.38, bf16[1,2048,1280]{2,1,0:T(8,128)(2,1)} %param.12), kind=kOutput, calls=%fused_computation.9 | convolution fusion | flops 23625728000 | bytes 126812160 | tf_op jit(solution)/shard_map/dot_general | solution.py:287
  362.9 29.5 %convolution_convert_fusion.3 = bf16[1280,4480]{1,0:T(8,128)(2,1)S(1)} fusion(bf16[2048,1280]{1,0:T(8,128)(2,1)} %get-tuple-element.36, bf16[2048,4480]{1,0:T(8,128)(2,1)} %get-tuple-element.43), kind=kOutput, calls=%fused_computation.15 | convolution fusion | flops 23493836800 | bytes 35061760 | tf_op jit(solution)/shard_map/dot_general | solution.py:295
  392.4 4.7 copy.23
  397.0 0.0 reduce-scatter.11.cloned.1.call-update
  397.0 0.0 reduce-scatter.9.cloned.1.call-start
  397.1 30.8 %convolution_convert_fusion.4 = bf16[1280,4480]{1,0:T(8,128)(2,1)S(1)} fusion(bf16[2048,1280]{1,0:T(8,128)(2,1)} %get-tuple-element.36, bf16[2048,4480]{1,0:T(8,128)(2,1)} %get-tuple-element.45), kind=kOutput, calls=%fused_computation.16 | convolution fusion | flops 23493836800 | bytes 35061760 | tf_op jit(solution)/shard_map/dot_general | solution.py:295
  427.9 4.7 copy.22
  432.6 0.0 reduce-scatter.9.cloned.1.call-update
  432.6 0.0 reduce-scatter.13.cloned.1.call-start
  432.7 0.0 reduce-scatter.11.cloned.1.call-done
  432.7 35.2 %fusion.46 = f32[2048,1280]{1,0:T(8,128)} fusion(bf16[2048,4480]{1,0:T(8,128)(2,1)} %get-tuple-element.43, bf16[1280,4480]{1,0:T(8,128)(2,1)} %get-tuple-element.44), kind=kOutput, calls=%fused_computation.89 | convolution fusion | flops 23488102400 | bytes 40304640 | tf_op jit(solution)/shard_map/dot_general | solution.py:299
  467.9 33.6 %fusion.21 = (f32[2048]{0:T(1024)S(1)}, f32[2048]{0:T(1024)S(1)}, bf16[2048,1280]{1,0:T(8,128)(2,1)}) fusion(bf16[2048,1280]{1,0:T(8,128)(2,1)} %get-tuple-element.47, f32[2048,1280]{1,0:T(8,128)} %fusion.46, bf16[2048,4480]{1,0:T(8,128)(2,1)} %get-tuple-element.45, bf16[1280,4480]{1,0:T(8,128)(2,1)} %get-tuple-element.46), kind=kOutput, calls=%fused_computation.52 | convolution fusion | flops 23509069824 | bytes 50806784 | tf_op jit(solution)/shard_map/dot_general | solution.py:299
  501.5 9.7 fusion.30
  511.2 28.8 %convolution_convert_fusion.5 = bf16[4480,1280]{1,0:T(8,128)(2,1)S(1)} fusion(bf16[2048,4480]{1,0:T(8,128)(2,1)} %get-tuple-element.35, bf16[2048,1280]{1,0:T(8,128)(2,1)} %fusion.30), kind=kOutput, calls=%fused_computation.17 | convolution fusion | flops 23493836800 | bytes 35061760 | tf_op jit(solution)/shard_map/dot_general | solution.py:295
  540.0 4.6 copy.26
  544.6 0.0 reduce-scatter.13.cloned.1.call-update
  544.7 0.0 reduce-scatter.15.cloned.1.call-start
  544.7 54.2 %fusion.2 = (bf16[2048,4480]{1,0:T(8,128)(2,1)}, bf16[2048,4480]{1,0:T(8,128)(2,1)}) fusion(f32[2048,4480]{1,0:T(8,128)} %get-tuple-element.51, f32[2048,4480]{1,0:T(8,128)} %get-tuple-element.50, bf16[2048,1280]{1,0:T(8,128)(2,1)} %fusion.30, bf16[4480,1280]{1,0:T(8,128)(2,1)} %get-tuple-element.49), kind=kOutput, calls=%fused_computation.4 | convolution fusion | flops 23625728000 | bytes 126812160 | tf_op jit(solution)/shard_map/dot_general | solution.py:287
  598.9 29.5 %convolution_convert_fusion.1 = bf16[1280,4480]{1,0:T(8,128)(2,1)S(1)} fusion(bf16[2048,1280]{1,0:T(8,128)(2,1)} %get-tuple-element.34, bf16[2048,4480]{1,0:T(8,128)(2,1)} %get-tuple-element.52), kind=kOutput, calls=%fused_computation.13 | convolution fusion | flops 23493836800 | bytes 35061760 | tf_op jit(solution)/shard_map/dot_general | solution.py:295
  628.3 4.7 copy.27
  633.0 0.0 reduce-scatter.15.cloned.1.call-update
  633.0 0.0 reduce-scatter.17.cloned.1.call-start
  633.1 30.6 %convolution_convert_fusion = bf16[1280,4480]{1,0:T(8,128)(2,1)S(1)} fusion(bf16[2048,1280]{1,0:T(8,128)(2,1)} %get-tuple-element.34, bf16[2048,4480]{1,0:T(8,128)(2,1)} %get-tuple-element.53), kind=kOutput, calls=%fused_computation.12 | convolution fusion | flops 23493836800 | bytes 35061760 | tf_op jit(solution)/shard_map/dot_general | solution.py:295
  663.7 4.7 copy.28
  668.4 0.0 reduce-scatter.17.cloned.1.call-update
  668.4 2.0 dynamic-slice_bitcast_fusion
  670.5 0.0 collective-permute-start.5
  670.5 4.2 dynamic-slice_bitcast_fusion.4
  674.7 2.0 collective-permute-start.1
  676.7 3.0 dynamic-slice_bitcast_fusion.2
  679.7 0.0 slice-start.4
  679.7 0.1 collective-permute-start.3
  679.8 2.6 dynamic-slice_bitcast_fusion.1
  682.4 2.3 collective-permute-start.4
  684.7 50.9 %collective-permute-done.5 = bf16[1120,1280]{1,0:T(8,128)(2,1)} collective-permute-done((bf16[1120,1280]{1,0:T(8,128)(2,1)S(1)}, bf16[1120,1280]{1,0:T(8,128)(2,1)}, u32[]{:S(2)}, u32[]{:S(2)}) %collective-permute-start.5) | collective-permute-done | bytes 2867232 | tf_op jit(solution)/shard_map/ppermute | solution.py:317
  735.6 3.4 fusion.38
  739.0 58.0 %collective-permute-done.1 = bf16[320,4480]{1,0:T(8,128)(2,1)} collective-permute-done((bf16[320,4480]{1,0:T(8,128)(2,1)}, bf16[320,4480]{1,0:T(8,128)(2,1)}, u32[]{:S(2)}, u32[]{:S(2)}) %collective-permute-start.1) | collective-permute-done | bytes 2867232 | tf_op jit(solution)/shard_map/ppermute | solution.py:317
  797.0 4.9 fusion.34
  801.9 56.4 %collective-permute-done.3 = bf16[320,4480]{1,0:T(8,128)(2,1)S(1)} collective-permute-done((bf16[320,4480]{1,0:T(8,128)(2,1)S(1)}, bf16[320,4480]{1,0:T(8,128)(2,1)S(1)}, u32[]{:S(2)}, u32[]{:S(2)}) %collective-permute-start.3) | collective-permute-done | bytes 2867232 | tf_op jit(solution)/shard_map/ppermute | solution.py:317
  858.4 2.2 fusion.36
  860.6 54.8 %collective-permute-done.4 = bf16[1120,1280]{1,0:T(8,128)(2,1)S(1)} collective-permute-done((bf16[1120,1280]{1,0:T(8,128)(2,1)S(1)}, bf16[1120,1280]{1,0:T(8,128)(2,1)S(1)}, u32[]{:S(2)}, u32[]{:S(2)}) %collective-permute-start.4) | collective-permute-done | bytes 2867232 | tf_op jit(solution)/shard_map/ppermute | solution.py:317
  915.4 2.5 fusion.37
  917.9 3.6 dynamic-slice_bitcast_fusion.5
  921.5 0.3 collective-permute-start
  921.8 23.1 %fusion.16 = (bf16[2,1120,1280]{2,1,0:T(8,128)(2,1)}, f32[2,1120,1280]{2,1,0:T(8,128)}, f32[2,1120,1280]{2,1,0:T(8,128)}) fusion(bf16[2,1120,1280]{2,1,0:T(8,128)(2,1)} %wd.1, bf16[1,1120,1280]{2,1,0:T(8,128)(2,1)S(1)} %fusion.38, bf16[1,1120,1280]{2,1,0:T(8,128)(2,1)} %fusion.37, f32[2,1120,1280]{2,1,0:T(8,128)} %param.21, f32[2,1120,1280]{2,1,0:T(8,128)} %param.18), kind=kLoop, calls=%fused_computation.47 | loop fusion | flops 54476800 | bytes 63078400 | tf_op jit(solution)/shard_map/convert_element_type | solution.py:274
  944.9 0.0 slice-start
  944.9 0.0 reduce-scatter.17.cloned.1.call-done
  944.9 0.0 copy-start.1
  945.0 3.7 dynamic-slice_bitcast_fusion.3
  948.7 1.7 collective-permute-start.2
  950.4 36.4 %collective-permute-done = bf16[320,4480]{1,0:T(8,128)(2,1)} collective-permute-done((bf16[320,4480]{1,0:T(8,128)(2,1)}, bf16[320,4480]{1,0:T(8,128)(2,1)}, u32[]{:S(2)}, u32[]{:S(2)}) %collective-permute-start) | collective-permute-done | bytes 2867232 | tf_op jit(solution)/shard_map/ppermute | solution.py:317
  986.8 3.5 fusion.33
  990.3 0.0 slice-start.3
  990.3 0.0 copy-start
  990.3 18.4 %fusion.8 = (bf16[2,320,4480]{2,1,0:T(8,128)(2,1)}, f32[2,320,4480]{2,1,0:T(8,128)}, f32[2,320,4480]{2,1,0:T(8,128)}) fusion(bf16[2,320,4480]{2,1,0:T(8,128)(2,1)S(1)} %bitcast.91, bf16[1,320,4480]{2,1,0:T(8,128)(2,1)S(1)} %copy-done.1, bf16[1,320,4480]{2,1,0:T(8,128)(2,1)S(1)} %fusion.33, f32[2,320,4480]{2,1,0:T(8,128)} %param.19, f32[2,320,4480]{2,1,0:T(8,128)} %param.16), kind=kLoop, calls=%fused_computation.39 | loop fusion | flops 54476800 | bytes 63078400 | tf_op jit(solution)/shard_map/convert_element_type | solution.py:274
  1008.8 34.1 %collective-permute-done.2 = bf16[320,4480]{1,0:T(8,128)(2,1)S(1)} collective-permute-done((bf16[320,4480]{1,0:T(8,128)(2,1)}, bf16[320,4480]{1,0:T(8,128)(2,1)S(1)}, u32[]{:S(2)}, u32[]{:S(2)}) %collective-permute-start.2) | collective-permute-done | bytes 2867232 | tf_op jit(solution)/shard_map/ppermute | solution.py:317
  1042.9 2.5 fusion.35
  1045.4 18.0 %fusion.12 = (bf16[2,320,4480]{2,1,0:T(8,128)(2,1)}, f32[2,320,4480]{2,1,0:T(8,128)}, f32[2,320,4480]{2,1,0:T(8,128)}) fusion(bf16[2,320,4480]{2,1,0:T(8,128)(2,1)S(1)} %bitcast.93, bf16[1,320,4480]{2,1,0:T(8,128)(2,1)S(1)} %copy-done, bf16[1,320,4480]{2,1,0:T(8,128)(2,1)S(1)} %fusion.35, f32[2,320,4480]{2,1,0:T(8,128)} %param.20, f32[2,320,4480]{2,1,0:T(8,128)} %param.17), kind=kLoop, calls=%fused_computation.43 | loop fusion | flops 54476800 | bytes 63078400 | tf_op jit(solution)/shard_map/convert_element_type | solution.py:274
  (24 shorter events, 0.1 us)
Async XLA Ops:
  7.2 355.7 %reduce-scatter.7.cloned.1.call-start = ((), (), s32[]{:S(2)}) async-start(), calls=%async_computation.6 | async-start | bytes 17203200 | tf_op jit(solution)/shard_map/reduce_scatter | solution.py:283
  309.6 123.1 %reduce-scatter.11.cloned.1.call-start = ((), (), s32[]{:S(2)}) async-start(), calls=%async_computation.8 | async-start | bytes 17203200 | tf_op jit(solution)/shard_map/reduce_scatter | solution.py:283
  397.0 114.2 %reduce-scatter.9.cloned.1.call-start = ((), (), s32[]{:S(2)}) async-start(), calls=%async_computation.7 | async-start | bytes 17203200 | tf_op jit(solution)/shard_map/reduce_scatter | solution.py:283
  432.6 166.3 %reduce-scatter.13.cloned.1.call-start = ((), (), s32[]{:S(2)}) async-start(), calls=%async_computation.9 | async-start | bytes 17203200 | tf_op jit(solution)/shard_map/reduce_scatter | solution.py:283
  544.7 373.2 %reduce-scatter.15.cloned.1.call-start = ((), (), s32[]{:S(2)}) async-start(), calls=%async_computation.10 | async-start | bytes 17203200 | tf_op jit(solution)/shard_map/reduce_scatter | solution.py:283
  633.0 311.9 %reduce-scatter.17.cloned.1.call-start = ((), (), s32[]{:S(2)}) async-start(), calls=%async_computation.11 | async-start | bytes 17203200 | tf_op jit(solution)/shard_map/reduce_scatter | solution.py:283
  670.5 65.1 %collective-permute-start.5 = (bf16[1120,1280]{1,0:T(8,128)(2,1)S(1)}, bf16[1120,1280]{1,0:T(8,128)(2,1)}, u32[]{:S(2)}, u32[]{:S(2)}) collective-permute-start(bf16[1120,1280]{1,0:T(8,128)(2,1)S(1)} %dynamic-slice_bitcast_fusion), channel_id=1, source_target_pairs={{0,2},{1,3},{2,0},{3,1},{4,6},{5,7},{6,4},{7,5}} | collective-permute-start | bytes 8601608 | tf_op jit(solution)/shard_map/ppermute | solution.py:317
  674.7 122.3 %collective-permute-start.1 = (bf16[320,4480]{1,0:T(8,128)(2,1)}, bf16[320,4480]{1,0:T(8,128)(2,1)}, u32[]{:S(2)}, u32[]{:S(2)}) collective-permute-start(bf16[320,4480]{1,0:T(8,128)(2,1)} %dynamic-slice_bitcast_fusion.4), channel_id=1, source_target_pairs={{0,2},{1,3},{2,0},{3,1},{4,6},{5,7},{6,4},{7,5}} | collective-permute-start | bytes 8601608 | tf_op jit(solution)/shard_map/ppermute | solution.py:317
  679.7 178.7 %slice-start.4 = ((s8[5734400]{0:T(1024)(128)(4,1)}), s8[4194304]{0:T(1024)(128)(4,1)S(1)}, s32[]{:S(2)}) async-start(s8[5734400]{0:T(1024)(128)(4,1)} %bitcast.105), calls=%async_computation.16 | async-start | bytes 8388608
  679.7 178.7 %collective-permute-start.3 = (bf16[320,4480]{1,0:T(8,128)(2,1)S(1)}, bf16[320,4480]{1,0:T(8,128)(2,1)S(1)}, u32[]{:S(2)}, u32[]{:S(2)}) collective-permute-start(bf16[320,4480]{1,0:T(8,128)(2,1)S(1)} %dynamic-slice_bitcast_fusion.2), channel_id=1, source_target_pairs={{0,2},{1,3},{2,0},{3,1},{4,6},{5,7},{6,4},{7,5}} | collective-permute-start | bytes 8601608 | tf_op jit(solution)/shard_map/ppermute | solution.py:317
  682.4 176.0 %slice-start.5 = ((s8[5734400]{0:T(1024)(128)(4,1)}), s8[1540096]{0:T(1024)(128)(4,1)S(1)}, s32[]{:S(2)}) async-start(s8[5734400]{0:T(1024)(128)(4,1)} %bitcast.105), calls=%async_computation.17 | async-start | bytes 3080192
  682.4 233.1 %slice-start.6 = ((s8[5734400]{0:T(1024)(128)(4,1)}), s8[4194304]{0:T(1024)(128)(4,1)S(1)}, s32[]{:S(2)}) async-start(s8[5734400]{0:T(1024)(128)(4,1)} %bitcast.113), calls=%async_computation.18 | async-start | bytes 8388608
  682.4 233.0 %collective-permute-start.4 = (bf16[1120,1280]{1,0:T(8,128)(2,1)S(1)}, bf16[1120,1280]{1,0:T(8,128)(2,1)S(1)}, u32[]{:S(2)}, u32[]{:S(2)}) collective-permute-start(bf16[1120,1280]{1,0:T(8,128)(2,1)S(1)} %dynamic-slice_bitcast_fusion.1), channel_id=1, source_target_pairs={{0,2},{1,3},{2,0},{3,1},{4,6},{5,7},{6,4},{7,5}} | collective-permute-start | bytes 8601608 | tf_op jit(solution)/shard_map/ppermute | solution.py:317
  739.0 176.5 %slice-start.7 = ((s8[5734400]{0:T(1024)(128)(4,1)}), s8[1540096]{0:T(1024)(128)(4,1)S(1)}, s32[]{:S(2)}) async-start(s8[5734400]{0:T(1024)(128)(4,1)} %bitcast.113), calls=%async_computation.19 | async-start | bytes 3080192
  921.5 65.3 %collective-permute-start = (bf16[320,4480]{1,0:T(8,128)(2,1)}, bf16[320,4480]{1,0:T(8,128)(2,1)}, u32[]{:S(2)}, u32[]{:S(2)}) collective-permute-start(bf16[320,4480]{1,0:T(8,128)(2,1)} %dynamic-slice_bitcast_fusion.5), channel_id=1, source_target_pairs={{0,2},{1,3},{2,0},{3,1},{4,6},{5,7},{6,4},{7,5}} | collective-permute-start | bytes 8601608 | tf_op jit(solution)/shard_map/ppermute | solution.py:317
  944.9 45.4 %slice-start = ((s8[5734400]{0:T(1024)(128)(4,1)}), s8[1540096]{0:T(1024)(128)(4,1)S(1)}, s32[]{:S(2)}) async-start(s8[5734400]{0:T(1024)(128)(4,1)} %bitcast.90), calls=%async_computation.12 | async-start | bytes 3080192
  944.9 45.3 %copy-start.1 = (bf16[1,320,4480]{2,1,0:T(8,128)(2,1)S(1)}, bf16[1,320,4480]{2,1,0:T(8,128)(2,1)}, u32[]{:S(2)}) copy-start(bf16[1,320,4480]{2,1,0:T(8,128)(2,1)} %fusion.34) | copy-start | bytes 8601604
  948.7 41.6 %slice-start.1 = ((s8[5734400]{0:T(1024)(128)(4,1)}), s8[4194304]{0:T(1024)(128)(4,1)S(1)}, s32[]{:S(2)}) async-start(s8[5734400]{0:T(1024)(128)(4,1)} %bitcast.90), calls=%async_computation.13 | async-start | bytes 8388608
  948.7 94.2 %collective-permute-start.2 = (bf16[320,4480]{1,0:T(8,128)(2,1)}, bf16[320,4480]{1,0:T(8,128)(2,1)S(1)}, u32[]{:S(2)}, u32[]{:S(2)}) collective-permute-start(bf16[320,4480]{1,0:T(8,128)(2,1)} %dynamic-slice_bitcast_fusion.3), channel_id=1, source_target_pairs={{0,2},{1,3},{2,0},{3,1},{4,6},{5,7},{6,4},{7,5}} | collective-permute-start | bytes 8601608 | tf_op jit(solution)/shard_map/ppermute | solution.py:317
  986.8 58.6 %slice-start.2 = ((s8[5734400]{0:T(1024)(128)(4,1)}), s8[4194304]{0:T(1024)(128)(4,1)S(1)}, s32[]{:S(2)}) async-start(s8[5734400]{0:T(1024)(128)(4,1)} %bitcast.92), calls=%async_computation.14 | async-start | bytes 8388608
  990.3 55.1 %slice-start.3 = ((s8[5734400]{0:T(1024)(128)(4,1)}), s8[1540096]{0:T(1024)(128)(4,1)S(1)}, s32[]{:S(2)}) async-start(s8[5734400]{0:T(1024)(128)(4,1)} %bitcast.92), calls=%async_computation.15 | async-start | bytes 3080192
  990.3 55.1 %copy-start = (bf16[1,320,4480]{2,1,0:T(8,128)(2,1)S(1)}, bf16[1,320,4480]{2,1,0:T(8,128)(2,1)}, u32[]{:S(2)}) copy-start(bf16[1,320,4480]{2,1,0:T(8,128)(2,1)} %fusion.36) | copy-start | bytes 8601604
Sparse Core Ops, SparseCore 0:
  309.7 16.3 reduce-scatter.6
  397.2 14.5 reduce-scatter.10
  432.7 15.6 reduce-scatter.8
  544.8 15.6 reduce-scatter.12
  633.1 15.6 reduce-scatter.14
  668.5 14.4 reduce-scatter.16
